TPU v7x, 512 devices: a whole 4x8x8 slice. The times are simulated.
512 devices in a mesh: row: 32 (over y_hi, x, core), col: 16 (over y_lo, z).
Axes of the slice: x: 4, y: 8 (y_hi: 4, y_lo: 2; y = y_hi * 2 + y_lo), z: 8, core: 2. Of those that a mesh axis runs over, the one named last changes fastest.
Arguments:
- amplitudes: bfloat16 [1024, 32768], P('row', 'col'), may hold values from -6 to 6
- integrals: bfloat16 [32768, 32768], P('col', 'row'), may hold values from -0.0390625 to 0.0390625
- tile_mask: int32 [256, 256], P('col', 'row'), may hold values 0 or 1
- driving: bfloat16 [1024, 32768], P('col', 'row'), may hold values from -6 to 6
- occupied_energy: float32 [1024], P('col'), may hold values from -1.5 to -0.5
- virtual_energy: float32 [32768], P('row'), may hold values from 0.5 to 2.5
Outputs:
- update: float32 [1024, 32768], P('col', 'row')
All inputs are finite; a program needn't handle non-finite values. No bound on the sum of `tile_mask` on one device may be relied on, other than what follows from the above.
Results may differ from a plain program's by a relative error of at most 0.0003.
Values may be sent and summed in bfloat16 or wider, within the bound.
A program may use at most 64 MiB of HBM per device.

v0:
```python
import jax
import jax.numpy as jnp
from jax import lax
from jax.sharding import PartitionSpec as P


def shards(amplitudes, integrals, tile_mask, driving, occupied_energy, virtual_energy):
    tiles_in = tile_mask.shape[0]
    tiles_out = tile_mask.shape[1]
    tile_size = integrals.shape[0] // tiles_in
    shaped = integrals.reshape(tiles_in, tile_size, tiles_out, tile_size)
    masked = (shaped * tile_mask.astype(jnp.bfloat16)[:, None, :, None]).reshape(integrals.shape)
    partial_sum = jnp.dot(
        lax.all_gather(amplitudes, "row", axis=0, tiled=True),
        masked,
        preferred_element_type=jnp.float32,
    )
    ladder = lax.psum_scatter(partial_sum, "col", scatter_dimension=0, tiled=True)
    denom = virtual_energy[None, :] - occupied_energy[:, None]
    return (driving.astype(jnp.float32) + ladder) / denom


def solution(mesh):
    in_specs = (
        P("row", "col"),
        P("col", "row"),
        P("col", "row"),
        P("col", "row"),
        P("col"),
        P("row"),
    )
    out_specs = P("col", "row")
    return jax.shard_map(shards, mesh=mesh, in_specs=in_specs, out_specs=out_specs, check_vma=False)
```

profile of v0, /device:TPU:2, one launch (start us, length us, event | category | flops | bytes accessed | tf_op | source)
XLA Modules:
  0.0 188.9 jit_solution(5905273928543527825)
XLA Ops:
  6.5 0.0 all-gather.2.cloned.1.call-start
  6.5 0.7 all-gather.2.cloned.1.call-update
  7.3 0.0 reduce-scatter.4.cloned.1.call-start
  7.3 0.7 convert_element_type.7
  8.0 0.1 copy.13
  8.1 72.6 %all-gather.2.cloned.1.call-done = bf16[1024,2048]{1,0:T(8,128)(2,1)} async-done(((bf16[32,2048]{1,0:T(8,128)(2,1)}), bf16[1024,2048]{1,0:T(8,128)(2,1)}) %all-gather.2.cloned.1.call-update) | async-done | bytes 4194320 | tf_op jit(solution)/shard_map/all_gather | solution.py:14
  80.7 0.0 copy-start.3
  80.7 0.6 mul.11
  81.3 1.6 copy-done.3
  82.9 8.8 %fusion.2 = f32[1024,1024]{0,1:T(8,128)} fusion(bf16[1024,2048]{1,0:T(8,128)(2,1)} %all-gather.2.cloned.1.call-done, bf16[2048,1024]{1,0:T(8,128)(2,1)S(1)} %copy-done.3, bf16[256,8,8,128]{3,2,1,0:T(8,128)(2,1)S(1)} %bitcast.11), kind=kOutput, calls=%fused_computation.3 | convolution fusion | flops 4297064448 | bytes 16777216 | tf_op jit(solution)/shard_map/dot_general | solution.py:13
  91.7 5.4 %copy.15 = f32[1024,1024]{1,0:T(8,128)} copy(f32[1024,1024]{0,1:T(8,128)} %fusion.2) | data formatting | bytes 8388608
  97.1 0.0 copy-start
  97.1 0.0 copy-start.1
  97.1 0.0 copy-start.2
  97.1 0.0 reduce-scatter.4.cloned.1.call-update
  97.1 83.2 %reduce-scatter.4.cloned.1.call-done = f32[64,1024]{1,0:T(8,128)} async-done(((f32[1024,1024]{1,0:T(8,128)}), f32[64,1024]{1,0:T(8,128)}) %reduce-scatter.4.cloned.1.call-update) | async-done | bytes 262160 | tf_op jit(solution)/shard_map/reduce_scatter | solution.py:18
  180.3 0.0 copy-done
  180.3 0.0 copy-done.1
  180.3 0.0 copy-done.2
  180.3 1.8 subtract_divide_fusion
Async XLA Ops:
  6.5 74.2 %all-gather.2.cloned.1.call-start = ((), (), s32[]{:S(2)}) async-start(), calls=%async_computation.1 | async-start | bytes 4325376 | tf_op jit(solution)/shard_map/all_gather | solution.py:14
  7.3 173.1 %reduce-scatter.4.cloned.1.call-start = ((), (), s32[]{:S(2)}) async-start(), calls=%async_computation.2 | async-start | bytes 4456448 | tf_op jit(solution)/shard_map/reduce_scatter | solution.py:18
  80.7 2.2 %copy-start.3 = (bf16[2048,1024]{1,0:T(8,128)(2,1)S(1)}, bf16[2048,1024]{1,0:T(8,128)(2,1)}, u32[]{:S(2)}) copy-start(bf16[2048,1024]{1,0:T(8,128)(2,1)} %param.7) | copy-start | bytes 12582916
  97.1 83.3 %copy-start = (bf16[64,1024]{1,0:T(8,128)(2,1)S(1)}, bf16[64,1024]{1,0:T(8,128)(2,1)}, u32[]{:S(2)}) copy-start(bf16[64,1024]{1,0:T(8,128)(2,1)} %param.9) | copy-start | bytes 393220
  97.1 83.3 %copy-start.1 = (f32[1024]{0:T(1024)S(1)}, f32[1024]{0:T(1024)}, u32[]{:S(2)}) copy-start(f32[1024]{0:T(1024)} %param.11) | copy-start | bytes 12292
  97.1 83.3 %copy-start.2 = (f32[64]{0:T(128)S(1)}, f32[64]{0:T(128)}, u32[]{:S(2)}) copy-start(f32[64]{0:T(128)} %param.10) | copy-start | bytes 772
Sparse Core Ops, SparseCore 0:
  10.5 70.1 all-gather.1
  97.2 83.0 reduce-scatter.3
where the time goes:
time: 189 us
  waiting for transfers between devices  157 us (83%)
  between operations  13.4 us (7%)
  matrix products  8.82 us (5%)
  local copies, waits for them, and re-layouts  7.65 us (4%)
  other arithmetic  2.45 us (1%)
    reduce_scatter x1, waiting for transfers between devices, shards(): lax.psum_scatter(partial_sum, 'col', scatter_dimension=0, tiled=True)  83.2 us
    all_gather x1, waiting for transfers between devices, shards(): lax.all_gather(amplitudes, 'row', axis=0, tiled=True)  72.6 us
    dot_general x1, matrix products, shards(): jnp.dot(lax.all_gather(amplitudes, 'row', axis=0, tiled=True), masked, pr...  8.82 us
    unnamed x9, local copies, waits for them, and re-layouts  6.95 us
  transfers between devices with their start and end apart: 2, of which 2 were waited for; matrix products, arithmetic and copies ran while one was open for 0% of the time, Pallas kernels for 0%

commit v1 on v0

--- a/solution.py
+++ b/solution.py
@@ -10,11 +10,10 @@
     tile_size = integrals.shape[0] // tiles_in
     shaped = integrals.reshape(tiles_in, tile_size, tiles_out, tile_size)
     masked = (shaped * tile_mask.astype(jnp.bfloat16)[:, None, :, None]).reshape(integrals.shape)
-    partial_sum = jnp.dot(
-        lax.all_gather(amplitudes, "row", axis=0, tiled=True),
-        masked,
-        preferred_element_type=jnp.float32,
+    seats_all_work = lambda along_dim, block_here: jnp.concatenate(
+        lax.all_to_all(jnp.stack([block_here] * lax.axis_size("row")), "row", 0, 0), along_dim
     )
+    partial_sum = jnp.dot(seats_all_work(0, amplitudes), masked, preferred_element_type=jnp.float32)
     ladder = lax.psum_scatter(partial_sum, "col", scatter_dimension=0, tiled=True)
     denom = virtual_energy[None, :] - occupied_energy[:, None]
     return (driving.astype(jnp.float32) + ladder) / denom

time: 189 us -> 228 us (1.21)
  the two profiles are of different devices: /device:TPU:2 before, /device:TPU:6 now
where the time goes in v1:
time: 228 us
  waiting for transfers between devices  182 us (80%)
  between operations  13.4 us (6%)
  local copies, waits for them, and re-layouts  11 us (5%)
  starting transfers between devices  10.5 us (5%)
  matrix products  8.89 us (4%)
    all_to_all x1, waiting for transfers between devices, shards(): lax.all_to_all(jnp.stack([block_here] * lax.axis_size('row')), 'row', 0, 0)  96.7 us
    reduce_scatter x1, waiting for transfers between devices, shards(): lax.psum_scatter(partial_sum, 'col', scatter_dimension=0, tiled=True)  85.8 us
    all_to_all x1, starting transfers between devices, shards(): lax.all_to_all(jnp.stack([block_here] * lax.axis_size('row')), 'row', 0, 0)  10.4 us
    dot_general x1, matrix products, shards(): jnp.dot(seats_all_work(0, amplitudes), masked, preferred_element_type=jnp...  8.89 us
    unnamed x11, local copies, waits for them, and re-layouts  6.94 us
  transfers between devices with their start and end apart: 2, of which 2 were waited for; matrix products, arithmetic and copies ran while one was open for 0% of the time, Pallas kernels for 0%

profile of v1, /device:TPU:6, one launch (start us, length us, event | category | flops | bytes accessed | tf_op | source)
XLA Modules:
  0.0 228.1 jit_solution(650126198629270228)
XLA Ops:
  6.5 3.4 %stack.2 = bf16[32,32,2048]{2,1,0:T(8,128)(2,1)} broadcast(bf16[32,2048]{1,0:T(8,128)(2,1)} %param.6), dimensions={1,2} | broadcast | bytes 4325376 | tf_op jit(solution)/shard_map/stack | solution.py:14
  9.9 0.0 copy-start.2
  9.9 10.4 %all-to-all-start = ((bf16[32,32,2048]{2,1,0:T(8,128)(2,1)}), bf16[32,32,2048]{2,1,0:T(8,128)(2,1)}, u32[]{:S(2)}, u32[]{:S(2)}) async-start(bf16[32,32,2048]{2,1,0:T(8,128)(2,1)} %stack.2), calls=%async_computation | async-start | bytes 8388608 | tf_op jit(solution)/shard_map/all_to_all | solution.py:14
  20.4 0.0 reduce-scatter.4.cloned.1.call-start
  20.4 0.0 copy-done.2
  20.5 0.1 copy.13
  20.5 96.7 %all-to-all-done = bf16[32,32,2048]{2,1,0:T(8,128)(2,1)} async-done(((bf16[32,32,2048]{2,1,0:T(8,128)(2,1)}), bf16[32,32,2048]{2,1,0:T(8,128)(2,1)}, u32[]{:S(2)}, u32[]{:S(2)}) %all-to-all-start) | async-done | bytes 4194336 | tf_op jit(solution)/shard_map/all_to_all | solution.py:14
  117.2 0.0 copy-start.4
  117.2 0.6 mul.11
  117.8 1.6 copy-done.4
  119.4 8.9 %fusion.2 = f32[1024,1024]{0,1:T(8,128)} fusion(bf16[1024,2048]{1,0:T(8,128)(2,1)} %bitcast, bf16[2048,1024]{1,0:T(8,128)(2,1)S(1)} %copy-done.4, bf16[256,8,8,128]{3,2,1,0:T(8,128)(2,1)S(1)} %bitcast.12), kind=kOutput, calls=%fused_computation.3 | convolution fusion | flops 4297064448 | bytes 16777216 | tf_op jit(solution)/shard_map/dot_general | solution.py:16
  128.3 5.4 %copy.15 = f32[1024,1024]{1,0:T(8,128)} copy(f32[1024,1024]{0,1:T(8,128)} %fusion.2) | data formatting | bytes 8388608
  133.6 0.0 copy-start
  133.6 0.0 copy-start.1
  133.6 0.0 copy-start.3
  133.6 0.0 reduce-scatter.4.cloned.1.call-update
  133.7 85.8 %reduce-scatter.4.cloned.1.call-done = f32[64,1024]{1,0:T(8,128)} async-done(((f32[1024,1024]{1,0:T(8,128)}), f32[64,1024]{1,0:T(8,128)}) %reduce-scatter.4.cloned.1.call-update) | async-done | bytes 262160 | tf_op jit(solution)/shard_map/reduce_scatter | solution.py:17
  219.4 0.0 copy-done
  219.5 0.0 copy-done.1
  219.5 0.0 copy-done.3
  219.5 1.8 subtract_divide_fusion
  (1 shorter events, 0.0 us)
Async XLA Ops:
  9.9 10.5 %copy-start.2 = (s32[16,8]{0,1:T(8,128)S(1)}, s32[16,8]{0,1:T(8,128)}, u32[]{:S(2)}) copy-start(s32[16,8]{0,1:T(8,128)} %param.8) | copy-start | bytes 1540
  9.9 107.3 %all-to-all-start = ((bf16[32,32,2048]{2,1,0:T(8,128)(2,1)}), bf16[32,32,2048]{2,1,0:T(8,128)(2,1)}, u32[]{:S(2)}, u32[]{:S(2)}) async-start(bf16[32,32,2048]{2,1,0:T(8,128)(2,1)} %stack.2), calls=%async_computation | async-start | bytes 8388608 | tf_op jit(solution)/shard_map/all_to_all | solution.py:14
  20.4 199.1 %reduce-scatter.4.cloned.1.call-start = ((), (), s32[]{:S(2)}) async-start(), calls=%async_computation.2 | async-start | bytes 4456448 | tf_op jit(solution)/shard_map/reduce_scatter | solution.py:17
  117.2 2.2 copy-start.4
  133.6 85.8 %copy-start = (bf16[64,1024]{1,0:T(8,128)(2,1)S(1)}, bf16[64,1024]{1,0:T(8,128)(2,1)}, u32[]{:S(2)}) copy-start(bf16[64,1024]{1,0:T(8,128)(2,1)} %param.9) | copy-start | bytes 393220
  133.6 85.8 %copy-start.1 = (f32[1024]{0:T(1024)S(1)}, f32[1024]{0:T(1024)}, u32[]{:S(2)}) copy-start(f32[1024]{0:T(1024)} %param.11) | copy-start | bytes 12292
  133.6 85.8 %copy-start.3 = (f32[64]{0:T(128)S(1)}, f32[64]{0:T(128)}, u32[]{:S(2)}) copy-start(f32[64]{0:T(128)} %param.10) | copy-start | bytes 772
Sparse Core Ops, SparseCore 0:
  133.8 85.6 reduce-scatter.3
